TPU v7x, 32 devices: a whole 2x2x4 slice. The times are simulated.
32 devices in a mesh: gx: 4 (over x, core), gy: 4 (over z), gz: 2 (over y).
Axes of the slice: x: 2, y: 2, z: 4, core: 2. Of those that a mesh axis runs over, the one named last changes fastest.
Arguments:
- hidden_rows: bfloat16 [2048, 16384], P(('gx', 'gy'), 'gz'), may hold values from -2000 to 2000
- norm_gain: bfloat16 [16384], P('gz'), may hold values from 0.5 to 1.5
- w_query: bfloat16 [16384, 16384], P('gz', ('gx', 'gy')), may hold values from -0.046875 to 0.046875
- w_keyval: bfloat16 [16384, 2048], P('gz', ('gx', 'gy')), may hold values from -0.046875 to 0.046875
- positions: int32 [2048], P('gz'), may hold values from 0 to 511, as said below
- keyval_order: int32 [8], replicated, may hold values from 0 to 7, each once
Outputs:
- queries: bfloat16 [2048, 16384], P('gz', ('gx', 'gy'))
- keyval_owned: bfloat16 [8, 2048, 256], P('gy', 'gz')
Inputs may be any that keep to these rules, and one draw needn't show every extreme that they name: `positions`: each token's position within its packed document: 0 where a document starts, else one more than the previous token's; a document holds at most 512 tokens. `keyval_order`: each head once.
All inputs are finite; a program needn't handle non-finite values.
Results may differ from a plain program's by a relative error of at most 0.0066.
Values may be sent and summed in bfloat16 or wider, within the bound.
A program may use at most 128 MiB of HBM per device.

v0:
```python
import math

import jax
import jax.numpy as jnp
from jax import lax
from jax.sharding import PartitionSpec as P

D = 16384
KVH = 8
HD = 128


rope_base = 500000.0
norm_eps = 1e-05


def rotate_pairs(values, position_ids, col_start, keys_only):
    row_total, col_width = values.shape
    pair_col = col_start + 2 * jnp.arange(col_width // 2, dtype=jnp.int32)
    within = pair_col % HD
    inv_freq = jnp.exp((within // 2).astype(jnp.float32) * (-2.0 * math.log(rope_base) / HD))
    angles = position_ids.astype(jnp.float32)[:, None] * inv_freq[None, :]
    cosines = jnp.cos(angles)
    sine_part = jnp.sin(angles)
    paired = values.reshape(row_total, col_width // 2, 2)
    even_part = paired[..., 0]
    odd_part = paired[..., 1]
    rotated = jnp.stack(
        [even_part * cosines - odd_part * sine_part, even_part * sine_part + odd_part * cosines],
        axis=-1,
    )
    if keys_only:
        is_key = (pair_col // HD % 2 == 0)[None, :, None]
        rotated = jnp.where(is_key, rotated, paired)
    return rotated.reshape(row_total, col_width)


def body(hidden_rows, norm_gain, w_query, w_keyval, positions, keyval_order):
    widened_gain = norm_gain.astype(jnp.float32)
    widened = hidden_rows.astype(jnp.float32)
    factor = lax.rsqrt(lax.psum(jnp.sum(widened * widened, axis=1), "gz") / D + norm_eps)
    normed_rows = (
        hidden_rows.astype(jnp.float32) * factor[:, None] * widened_gain[None, :]
    ).astype(jnp.bfloat16)
    query_width = w_query.shape[1]
    keyval_width = w_keyval.shape[1]
    group_size = lax.axis_size("gy")
    gathered = lax.all_gather(normed_rows, ("gx", "gy"), axis=0, tiled=True)
    query_sum = lax.psum_scatter(
        jnp.dot(gathered, w_query, preferred_element_type=jnp.float32),
        "gz",
        scatter_dimension=0,
        tiled=True,
    )
    keyval_sum = lax.psum_scatter(
        jnp.dot(gathered, w_keyval, preferred_element_type=jnp.float32),
        "gz",
        scatter_dimension=0,
        tiled=True,
    )
    col_index = lax.axis_index("gx") * group_size + lax.axis_index("gy")
    queries = rotate_pairs(query_sum, positions, col_index * query_width, False).astype(
        jnp.bfloat16
    )
    keyval_part = rotate_pairs(keyval_sum, positions, col_index * keyval_width, True).astype(
        jnp.bfloat16
    )
    keyval_all = lax.all_gather(keyval_part, ("gx", "gy"), axis=1, tiled=True)
    slot_count = KVH // group_size
    first_slot = lax.axis_index("gy") * slot_count
    keyval_heads = keyval_all.reshape(keyval_all.shape[0], KVH, 2 * HD)
    wanted = lax.dynamic_slice_in_dim(keyval_order, first_slot, slot_count, 0)
    selector = (wanted[:, None] == jnp.arange(KVH, dtype=jnp.int32)[None, :]).astype(jnp.bfloat16)
    keyval_owned = jnp.einsum(
        "sh,rhc->src", selector, keyval_heads, preferred_element_type=jnp.float32
    ).astype(jnp.bfloat16)
    return (queries, keyval_owned)


def solution(mesh):
    in_specs = (
        P(("gx", "gy"), "gz"),
        P("gz"),
        P("gz", ("gx", "gy")),
        P("gz", ("gx", "gy")),
        P("gz"),
        P(),
    )
    out_specs = (P("gz", ("gx", "gy")), P("gy", "gz", None))
    return jax.shard_map(body, mesh=mesh, in_specs=in_specs, out_specs=out_specs, check_vma=False)
```

profile of v0, /device:TPU:0, one launch (start us, length us, event | category | flops | bytes accessed | tf_op | source)
XLA Modules:
  0.0 452.2 jit_solution(973165586577102964)
XLA Ops:
  7.2 0.0 copy-start
  7.2 0.0 all-gather.3.cloned.1.call-start
  7.2 0.9 convert_element_type.40
  8.1 2.1 fusion
  10.2 5.9 %psum.7 = f32[128]{0:T(128)S(1)} all-reduce(f32[128]{0:T(128)S(1)} %fusion), channel_id=1, replica_groups=mesh['gx'=4,'gy'=4,'gz'=2] {'gz'}, use_global_device_ids=true, to_apply=%region_1.0 | all-reduce | flops 128 | bytes 1024 | tf_op jit(solution)/shard_map/psum | solution.py:41
  16.1 3.5 fusion.2
  19.6 0.0 all-gather.3.cloned.1.call-update
  19.6 0.0 copy-start.3
  19.6 0.0 reduce-scatter.5.cloned.1.call-start
  19.6 179.7 %all-gather.3.cloned.1.call-done = bf16[2048,8192]{1,0:T(8,128)(2,1)} async-done(((bf16[128,8192]{1,0:T(8,128)(2,1)}), bf16[2048,8192]{1,0:T(8,128)(2,1)}) %all-gather.3.cloned.1.call-update) | async-done | bytes 33554448 | tf_op jit(solution)/shard_map/all_gather | solution.py:48
  199.4 0.0 copy-done
  199.4 16.0 %fusion.32 = f32[2048,128]{1,0:T(8,128)} fusion(bf16[2048,8192]{1,0:T(8,128)(2,1)} %all-gather.3.cloned.1.call-done, bf16[8192,128]{1,0:T(8,128)(2,1)S(1)} %copy-done), kind=kOutput, calls=%fused_computation.65 | convolution fusion | flops 4294967296 | bytes 36700160 | tf_op jit(solution)/shard_map/dot_general | solution.py:56
  215.4 0.0 reduce-scatter.5.cloned.1.call-update
  215.4 0.0 all-gather.5.cloned.1.call-start
  215.5 0.0 copy-done.3
  215.5 0.1 broadcast_in_dim.9
  215.6 0.2 broadcast_in_dim.13
  215.8 20.2 %reduce-scatter.5.cloned.1.call-done = f32[1024,128]{1,0:T(8,128)} async-done(((f32[2048,128]{1,0:T(8,128)}), f32[1024,128]{1,0:T(8,128)}) %reduce-scatter.5.cloned.1.call-update) | async-done | bytes 524304 | tf_op jit(solution)/shard_map/reduce_scatter | solution.py:55
  236.0 1.2 copy.18
  237.2 0.3 reshape.298
  237.5 0.0 copy-start.2
  237.5 0.4 fusion.30
  238.0 1.2 fusion.15
  239.2 0.3 copy.21
  239.5 0.1 stack.15
  239.6 0.2 copy.22
  239.7 0.0 copy-done.2
  239.7 0.8 select_convert_fusion
  240.5 0.0 all-gather.5.cloned.1.call-update
  240.5 0.2 reduce-scatter.3.cloned.1.call-start
  240.8 43.4 %fusion.31 = f32[2048,1024]{1,0:T(8,128)} fusion(bf16[2048,8192]{1,0:T(8,128)(2,1)} %all-gather.3.cloned.1.call-done, bf16[8192,1024]{1,0:T(8,128)(2,1)} %param.8), kind=kOutput, calls=%fused_computation.64 | convolution fusion | flops 34359738368 | bytes 58720256 | tf_op jit(solution)/shard_map/dot_general | solution.py:50
  284.2 0.0 copy-start.4
  284.2 0.0 reduce-scatter.3.cloned.1.call-update
  284.2 0.6 copy-done.4
  284.8 0.1 dynamic_slice.3
  284.9 8.2 %all-gather.5.cloned.1.call-done = bf16[1024,2048]{1,0:T(8,128)(2,1)} async-done(((bf16[1024,128]{1,0:T(8,128)(2,1)}), bf16[1024,2048]{1,0:T(8,128)(2,1)}) %all-gather.5.cloned.1.call-update) | async-done | bytes 4194320 | tf_op jit(solution)/shard_map/all_gather | solution.py:68
  293.2 3.7 copy.29
  296.8 1.3 convolution_convert_fusion
  298.2 1.1 copy.24
  299.3 93.6 %reduce-scatter.3.cloned.1.call-done = f32[1024,1024]{1,0:T(8,128)} async-done(((f32[2048,1024]{1,0:T(8,128)}), f32[1024,1024]{1,0:T(8,128)}) %reduce-scatter.3.cloned.1.call-update) | async-done | bytes 4194320 | tf_op jit(solution)/shard_map/reduce_scatter | solution.py:49
  392.9 5.4 %copy.14 = f32[1024,1024]{0,1:T(8,128)} copy(f32[1024,1024]{1,0:T(8,128)} %reduce-scatter.3.cloned.1.call-done) | data formatting | bytes 8388608 | tf_op jit(solution)/shard_map/reduce_scatter | solution.py:49
  398.2 5.8 %reshape.297 = f32[1024,512,2]{0,2,1:T(2,128)} reshape(f32[1024,1024]{0,1:T(8,128)} %copy.14) | data formatting | bytes 8388608 | tf_op jit(solution)/shard_map/reshape | solution.py:25
  404.1 9.1 %fusion.29 = (f32[1024,512,1]{0,2,1:T(1,128)}, f32[1024,512,1]{0,2,1:T(1,128)}) fusion(f32[1024,512,2]{0,2,1:T(2,128)} %reshape.297), kind=kLoop, calls=%fused_computation.62 | loop fusion | bytes 8388608 | tf_op jit(solution)/shard_map/slice | solution.py:27
  413.1 4.6 %copy.25 = f32[1024,512,1]{1,0,2:T(8,128)S(1)} copy(f32[1024,512,1]{0,2,1:T(1,128)} %get-tuple-element.11) | data formatting | bytes 4194304
  417.7 6.0 %copy.26 = f32[1024,512,1]{1,0,2:T(8,128)} copy(f32[1024,512,1]{0,2,1:T(1,128)} %get-tuple-element.10) | data formatting | bytes 4194304
  423.7 9.5 %fusion.8 = (bf16[1024,512,1]{1,0,2:T(8,128)(2,1)S(1)}, bf16[1024,512,1]{1,0,2:T(8,128)(2,1)S(1)}) fusion(f32[1024,512,1]{1,0,2:T(8,128)} %copy.26, f32[1024,512,1]{1,0,2:T(8,128)S(1)} %copy.25, f32[512]{0:T(512)S(1)} %fusion.21, f32[1024]{0:T(1024)S(1)} %convert_element_type.42), kind=kLoop, calls=%fused_computation.12 | loop fusion | flops 4718592 | bytes 6297600 | tf_op jit(solution)/shard_map/convert
  433.3 0.2 pad_maximum_fusion
  433.5 3.9 copy.17
  437.4 0.0 copy-start.1
  437.5 4.3 convert_element_type.44
  441.7 3.9 copy.23
  445.6 0.0 copy-done.1
  (6 shorter events, 0.1 us)
Async XLA Ops:
  7.2 192.2 %copy-start = (bf16[8192,128]{1,0:T(8,128)(2,1)S(1)}, bf16[8192,128]{1,0:T(8,128)(2,1)}, u32[]{:S(2)}) copy-start(bf16[8192,128]{1,0:T(8,128)(2,1)} %param.9) | copy-start | bytes 6291460
  7.2 192.2 %all-gather.3.cloned.1.call-start = ((), (), s32[]{:S(2)}) async-start(), calls=%async_computation.2 | async-start | bytes 35651584 | tf_op jit(solution)/shard_map/all_gather | solution.py:48
  19.6 195.9 %copy-start.3 = (s32[1024]{0:T(1024)S(1)}, s32[1024]{0:T(1024)}, u32[]{:S(2)}) copy-start(s32[1024]{0:T(1024)} %param.10) | copy-start | bytes 12292
  19.6 216.4 %reduce-scatter.5.cloned.1.call-start = ((), (), s32[]{:S(2)}) async-start(), calls=%async_computation.4 | async-start | bytes 1572864 | tf_op jit(solution)/shard_map/reduce_scatter | solution.py:55
  215.4 77.7 %all-gather.5.cloned.1.call-start = ((), (), s32[]{:S(2)}) async-start(), calls=%async_computation.5 | async-start | bytes 4456448 | tf_op jit(solution)/shard_map/all_gather | solution.py:68
  237.5 2.2 copy-start.2
  240.5 152.3 %reduce-scatter.3.cloned.1.call-start = ((), (), s32[]{:S(2)}) async-start(), calls=%async_computation.3 | async-start | bytes 12582912 | tf_op jit(solution)/shard_map/reduce_scatter | solution.py:49
  284.2 0.7 copy-start.4
  437.4 8.2 %copy-start.1 = (bf16[8192,128]{1,0:T(8,128)(2,1)S(1)}, bf16[8192,128]{1,0:T(8,128)(2,1)}, u32[]{:S(2)}) copy-start(bf16[8192,128]{1,0:T(8,128)(2,1)} %param.9) | copy-start | bytes 6291460
Sparse Core Ops, SparseCore 0:
  19.7 179.6 all-gather.2
  215.6 20.3 reduce-scatter.4
  240.7 52.4 all-gather.4
  295.3 97.4 reduce-scatter.2
where the time goes:
time: 453 us; the launch traced here: 452 us
  waiting for transfers between devices  302 us (67%)
  matrix products  60.8 us (13%)
  local copies, waits for them, and re-layouts  51.2 us (11%)
  other arithmetic  18.2 us (4%)
  between operations  13.9 us (3%)
  blocking collectives  5.9 us (1%)
    all_gather x1, waiting for transfers between devices, body(): gathered = lax.all_gather(normed_rows, ('gx', 'gy'), axis=0, tiled=True)  180 us
    reduce_scatter x1, waiting for transfers between devices, body(): lax.psum_scatter(jnp.dot(gathered, w_query, preferred_element_type=jnp.fl...  93.6 us
    dot_general x1, matrix products, body(): jnp.dot(gathered, w_query, preferred_element_type=jnp.float32)  43.4 us
    reduce_scatter x1, waiting for transfers between devices, body(): lax.psum_scatter(jnp.dot(gathered, w_keyval, preferred_element_type=jnp.f...  20.2 us
    unnamed x15, local copies, waits for them, and re-layouts  20 us
    dot_general x1, matrix products, body(): jnp.dot(gathered, w_keyval, preferred_element_type=jnp.float32)  16 us
    another operation x1, other arithmetic  9.55 us
    slice x1, local copies, waits for them, and re-layouts, rotate_pairs(): odd_part = paired[..., 1]  9.07 us
  transfers between devices with their start and end apart: 4, of which 4 were waited for; matrix products, arithmetic and copies ran while one was open for 11% of the time, Pallas kernels for 0%

commit v1 on v0

v1 whole, which is shorter than its diff:
```python
import functools
import math

import jax
import jax.numpy as jnp
from jax import lax
from jax.experimental import pallas as pl
from jax.experimental.pallas import tpu as pltpu
from jax.sharding import PartitionSpec as P

HD = 128
CHUNKS = 1

rope_base = 500000.0
norm_eps = 1e-05


def swap_pairs(values):
    even = (jnp.arange(values.shape[-1]) % 2 == 0)
    return jnp.where(even, jnp.roll(values, -1, axis=-1), jnp.roll(values, 1, axis=-1))


def tables(position_ids, cols, row_scale, is_key):
    within = cols % HD
    inv_freq = jnp.exp((within // 2).astype(jnp.float32) * (-2.0 * math.log(rope_base) / HD))
    angles = position_ids.astype(jnp.float32)[:, None] * inv_freq[None, :]
    sign = jnp.where(cols % 2 == 0, -1.0, 1.0).astype(jnp.float32)[None, :]
    own = jnp.cos(angles)
    other = jnp.sin(angles) * sign
    if is_key is not None:
        own = jnp.where(is_key[None, :], own, 1.0)
        other = jnp.where(is_key[None, :], other, 0.0)
    return own * row_scale[:, None], other * row_scale[:, None]


def rotate_kernel(count, *refs):
    mine_ref = refs[0]
    got_refs = refs[1 : 1 + count]
    own_ref, other_ref = refs[1 + count], refs[2 + count]
    out_ref = refs[-1]
    groups, rows, width = mine_ref.shape
    for group in range(groups):
        own = own_ref[group, 0]
        other = other_ref[group, 0]
        even = lax.broadcasted_iota(jnp.int32, (rows, HD), 1) % 2 == 0
        for head in range(width // HD):
            cols = slice(head * HD, (head + 1) * HD)
            total = mine_ref[group, :, cols]
            for got in got_refs:
                total = total + got[group, :, cols].astype(jnp.float32)
            swapped = jnp.where(even, pltpu.roll(total, HD - 1, 1), pltpu.roll(total, 1, 1))
            out_ref[group, 0, :, cols] = (total * own + swapped * other).astype(out_ref.dtype)


def rotate_into(out, index, chunks, mine, got, own, other):
    groups, rows, width = mine.shape
    step = 2 if groups % 2 == 0 else 1
    part = pl.BlockSpec((step, rows, width), lambda i: (i, 0, 0))
    table = pl.BlockSpec((step, 1, rows, HD), lambda i: (i, index, 0, 0))
    operands = [mine, *got, own, other]
    specs = [part] * (1 + len(got)) + [table] * 2
    alias = {}
    if out is not None:
        alias = {len(operands): 0}
        operands.append(out)
        specs.append(pl.BlockSpec(memory_space=pl.ANY))
    return pl.pallas_call(
        functools.partial(rotate_kernel, len(got)),
        grid=(groups // step,),
        out_shape=jax.ShapeDtypeStruct((groups, chunks, rows, width), jnp.bfloat16),
        in_specs=specs,
        out_specs=pl.BlockSpec((step, 1, rows, width), lambda i: (i, index, 0, 0)),
        input_output_aliases=alias,
        name="rotate_rows",
        cost_estimate=pl.CostEstimate(
            flops=6 * mine.size, bytes_accessed=8 * mine.size, transcendentals=0
        ),
    )(*operands)


def body(hidden_rows, norm_gain, w_query, w_keyval, positions, keyval_order):
    sums = lax.axis_size("gz")
    me = lax.axis_index("gz")
    holders = lax.axis_size("gx") * lax.axis_size("gy")
    group_size = lax.axis_size("gy")
    rows, depth = hidden_rows.shape
    kv_width = w_keyval.shape[1]
    q_width = w_query.shape[1]
    chunks = CHUNKS
    part = rows // chunks
    groups = holders // sums
    gain = norm_gain.astype(jnp.float32)
    col_index = lax.axis_index("gx") * group_size + lax.axis_index("gy")

    gathered = []
    for c in range(chunks):
        piece = hidden_rows[c * part : (c + 1) * part]
        piece = (piece.astype(jnp.float32) * gain[None, :]).astype(jnp.bfloat16)
        gathered.append(lax.all_gather(piece, ("gx", "gy"), axis=0, tiled=True))

    widened = hidden_rows.astype(jnp.float32)
    squares = lax.all_gather(jnp.sum(widened * widened, axis=1), ("gx", "gy", "gz"), axis=0)
    squares = jnp.sum(squares.reshape(holders, sums, rows), axis=1).reshape(holders * rows)
    tokens = holders * rows // sums
    squares = lax.dynamic_slice_in_dim(squares, me * tokens, tokens, 0)
    factor = lax.rsqrt(squares / (depth * sums) + norm_eps)

    q_own, q_other = tables(positions, jnp.arange(HD, dtype=jnp.int32), factor, None)
    q_own = q_own.reshape(groups, chunks, part, HD)
    q_other = q_other.reshape(groups, chunks, part, HD)
    kv_cols = col_index * kv_width + jnp.arange(kv_width, dtype=jnp.int32)
    kv_own, kv_other = tables(positions, kv_cols, factor, kv_cols // HD % 2 == 0)
    kv_own = kv_own.reshape(groups, chunks, part, kv_width)
    kv_other = kv_other.reshape(groups, chunks, part, kv_width)

    def shifts(k):
        return [(i, (i + k) % sums) for i in range(sums)]

    def segment(block, k):
        size = groups * part
        return lax.dynamic_slice_in_dim(block, lax.rem(me + k, sums) * size, size, 0)

    out = None
    keyvals = []
    for c in range(chunks):
        block = gathered[c]
        kv_all = jnp.dot(block, w_keyval, preferred_element_type=jnp.float32)
        kv = segment(kv_all, 0)
        for k in range(1, sums):
            sent = segment(kv_all, k).astype(jnp.bfloat16)
            kv = kv + lax.ppermute(sent, "gz", shifts(k)).astype(jnp.float32)
        kv = kv.reshape(groups, part, kv_width)
        kv = (kv * kv_own[:, c] + swap_pairs(kv) * kv_other[:, c]).astype(jnp.bfloat16)
        keyvals.append(kv)

        got = []
        for k in range(1, sums):
            sent = jnp.dot(
                segment(block, k), w_query, preferred_element_type=jnp.float32
            ).astype(jnp.bfloat16)
            got.append(lax.ppermute(sent, "gz", shifts(k)).reshape(groups, part, q_width))
        mine = jnp.dot(segment(block, 0), w_query, preferred_element_type=jnp.float32)
        mine = mine.reshape(groups, part, q_width)
        out = rotate_into(out, c, chunks, mine, got, q_own, q_other)
    queries = out.reshape(tokens, q_width)

    slot_count = keyval_order.shape[0] // group_size
    wanted = lax.dynamic_slice_in_dim(
        keyval_order, lax.axis_index("gy") * slot_count, slot_count, 0
    )
    half = chunks // 2
    owned = []
    for some in filter(len, (keyvals[:half], keyvals[half:])):
        stacked = jnp.stack(some, axis=1)
        full = lax.all_gather(stacked, ("gx", "gy"), axis=0)
        full = full.reshape(keyval_order.shape[0], -1, *stacked.shape)
        picked = jnp.stack(
            [lax.dynamic_index_in_dim(full, wanted[s], 0, False) for s in range(slot_count)]
        )
        picked = jnp.moveaxis(picked, 1, -2)
        owned.append(picked.reshape(*picked.shape[:-2], -1))
    keyval_owned = jnp.concatenate(owned, axis=2).reshape(slot_count, tokens, 2 * HD)
    return (queries, keyval_owned)


def solution(mesh):
    in_specs = (
        P(("gx", "gy"), "gz"),
        P("gz"),
        P("gz", ("gx", "gy")),
        P("gz", ("gx", "gy")),
        P("gz"),
        P(),
    )
    out_specs = (P("gz", ("gx", "gy")), P("gy", "gz", None))
    return jax.shard_map(body, mesh=mesh, in_specs=in_specs, out_specs=out_specs, check_vma=False)
```

time: 453 us -> 308 us (0.68)
  waiting for transfers between devices: 302 us -> 132 us
  blocking collectives: 5.9 us -> 70.7 us
  local copies, waits for them, and re-layouts: 51.2 us -> 7.38 us
  other arithmetic: 18.2 us -> 10.9 us
  Pallas kernels: 0 us -> 5.93 us
    reduce_scatter x2 -> x0, waiting for transfers between devices: 114 us -> none  [the longest x1 93.6 us: body(): lax.psum_scatter(jnp.dot(gathered, w_query, preferred_element_type=jnp.fl...]
    all_gather x2, waiting for transfers between devices: 188 us -> 109 us  [the longest x1 109 us: body(): gathered.append(lax.all_gather(piece, ('gx', 'gy'), axis=0, tiled=True))]
    all_gather x0 -> x1, blocking collectives: none -> 70.7 us  [body(): lax.all_gather(jnp.sum(widened * widened, axis=1), ('gx', 'gy', 'gz'), ax...]
    ppermute x0 -> x2, waiting for transfers between devices: none -> 22.6 us  [the longest x1 22.6 us: body(): lax.ppermute(sent, 'gz', shifts(k)).reshape(groups, part, q_width)]
    unnamed x15 -> x12, local copies, waits for them, and re-layouts: 20 us -> 1.73 us
    another operation x3 -> x0, other arithmetic: 9.77 us -> none
    slice x2, local copies, waits for them, and re-layouts: 9.48 us -> 0.87 us  [the longest x1 0.66 us: body(): wanted[s]]
    reduce_scatter x2 -> x0, local copies, waits for them, and re-layouts: 6.61 us -> none  [the longest x1 5.38 us: body(): lax.psum_scatter(jnp.dot(gathered, w_query, preferred_element_type=jnp.fl...]
  transfers between devices with their start and end apart: 4 -> 4, of which waited for: 4 -> 2; matrix products, arithmetic and copies ran while one was open for 11% -> 16% of each run, Pallas kernels for 0% -> 2%
where the time goes in v1:
time: 308 us
  waiting for transfers between devices  132 us (43%)
  blocking collectives  70.7 us (23%)
  matrix products  60.1 us (20%)
  between operations  18.2 us (6%)
  other arithmetic  10.9 us (4%)
  local copies, waits for them, and re-layouts  7.38 us (2%)
  Pallas kernels  5.93 us (2%)
    all_gather x1, waiting for transfers between devices, body(): gathered.append(lax.all_gather(piece, ('gx', 'gy'), axis=0, tiled=True))  109 us
    all_gather x1, blocking collectives, body(): lax.all_gather(jnp.sum(widened * widened, axis=1), ('gx', 'gy', 'gz'), ax...  70.7 us
    dot_general x1, matrix products, body(): jnp.dot(segment(block, 0), w_query, preferred_element_type=jnp.float32)  23.5 us
    ppermute x1, waiting for transfers between devices, body(): lax.ppermute(sent, 'gz', shifts(k)).reshape(groups, part, q_width)  22.6 us
    dot_general x1, matrix products, body(): jnp.dot(segment(block, k), w_query, preferred_element_type=jnp.float32)  21.9 us
    dot_general x1, matrix products, body(): kv_all = jnp.dot(block, w_keyval, preferred_element_type=jnp.float32)  14.7 us
  transfers between devices with their start and end apart: 4, of which 2 were waited for; matrix products, arithmetic and copies ran while one was open for 16% of the time, Pallas kernels for 2%

profile of v1, /device:TPU:0, one launch (start us, length us, event | category | flops | bytes accessed | tf_op | source)
XLA Modules:
  0.0 308.2 jit_solution(16480498006635234194)
XLA Ops:
  7.2 0.0 copy-start
  7.2 0.0 copy-start.4
  7.2 0.0 copy-start.3
  7.2 0.0 all-gather.5.cloned.1.call-start
  7.2 0.9 convert_element_type.48
  8.1 3.5 %fusion.5 = (f32[128]{0:T(128)S(1)}, bf16[128,8192]{1,0:T(8,128)(2,1)}) fusion(bf16[128,8192]{1,0:T(8,128)(2,1)} %param.6, f32[8192]{0:T(1024)S(1)} %convert_element_type.48), kind=kLoop, calls=%fused_computation.7 | loop fusion | flops 5242752 | bytes 4227584 | tf_op jit(solution)/shard_map/reduce_sum | solution.py:102
  11.6 0.0 all-gather.5.cloned.1.call-update
  11.7 0.0 all-gather.7.cloned.1.call-start
  11.7 70.7 %all-gather.1 = f32[32,1,128]{2,1,0:T(1,128)S(1)} all-gather(f32[1,1,128]{2,1,0:T(1,128)S(1)} %bitcast.48), channel_id=2, replica_groups=mesh['gx'=4,'gy'=4,'gz'=2] {'gx','gy','gz'}, dimensions={0}, use_global_device_ids=true | all-gather | bytes 16896 | tf_op jit(solution)/shard_map/all_gather | solution.py:102
  82.5 0.0 copy-done.4
  82.5 0.1 dynamic_slice.30
  82.6 0.7 fusion.29
  83.3 0.0 copy-done.3
  83.3 109.2 %all-gather.5.cloned.1.call-done = bf16[2048,8192]{1,0:T(8,128)(2,1)} async-done(((bf16[128,8192]{1,0:T(8,128)(2,1)}), bf16[2048,8192]{1,0:T(8,128)(2,1)}) %all-gather.5.cloned.1.call-update) | async-done | bytes 33554448 | tf_op jit(solution)/shard_map/all_gather | solution.py:99
  192.5 0.0 copy-done
  192.5 14.7 %fusion.30 = f32[2048,128]{1,0:T(8,128)S(1)} fusion(bf16[2048,8192]{1,0:T(8,128)(2,1)} %all-gather.5.cloned.1.call-done, bf16[8192,128]{1,0:T(8,128)(2,1)S(1)} %copy-done), kind=kOutput, calls=%fused_computation.69 | convolution fusion | flops 4294967296 | bytes 36700160 | tf_op jit(solution)/shard_map/dot_general | solution.py:127
  207.3 1.6 collective-permute-start.1
  212.9 3.1 %fusion.11 = (f32[8,1,128,128]{3,2,1,0:T(8,128)}, f32[8,1,128,128]{3,2,1,0:T(8,128)}) fusion(f32[128]{0:T(128)S(1)} %get-tuple-element.19, f32[8,128]{1,0:T(8,128)S(1)} %rsqrt_bitcast_fusion, f32[128]{0:T(128)S(1)} %get-tuple-element.18, f32[8,128]{1,0:T(8,128)S(1)} %convert_bitcast_fusion), kind=kLoop, calls=%fused_computation.16 | loop fusion | flops 524288 | bytes 1057792 | tf_op jit(solution)/shard_map/mul | solution.py:33
  216.0 0.0 collective-permute-done.1
  216.0 0.1 convert_add_fusion
  216.0 0.2 fusion.28
  216.2 0.2 slice_bitcast_fusion
  216.4 0.2 copy.25
  216.6 0.2 copy.20
  216.9 0.2 copy.26
  217.1 0.2 copy.22
  217.3 3.2 %fusion.16 = bf16[1,8,1,128,128]{4,3,2,1,0:T(8,128)(2,1)} fusion(f32[1,8,1,128,128]{4,3,2,1,0:T(8,128)S(1)} %bitcast.39, f32[1,8,1,128,1]{4,3,1,2,0:T(8,128)S(1)} %copy.20, f32[1,8,1,128,127]{4,3,1,2,0:T(8,128)S(1)} %get-tuple-element.9, f32[1,8,1,128,127]{4,3,2,1,0:T(8,128)S(1)} %get-tuple-element.8, f32[1,8,1,128,1]{4,3,2,1,0:T(8,128)S(1)} %copy.22, ...), kind=kLoop, calls=%fused_computation.21 | loop fusion | flops 1703936 | bytes 1844480 | tf_op jit(solution)/shard_map/convert_element_type | solution.py:133
  220.5 0.0 all-gather.7.cloned.1.call-update
  220.5 21.9 %fusion.6 = bf16[1024,1024]{1,0:T(8,128)(2,1)S(1)} fusion(bf16[8192,1024]{1,0:T(8,128)(2,1)} %param.8, bf16[2048,8192]{1,0:T(8,128)(2,1)} %all-gather.5.cloned.1.call-done, s32[]{:T(128)S(6)} %select_n.141), kind=kOutput, calls=%fused_computation.8 | convolution fusion | flops 17180917760 | bytes 35651588 | tf_op jit(solution)/shard_map/dot_general | solution.py:138
  242.4 1.4 collective-permute-start
  243.8 23.5 %fusion.2 = f32[1024,1024]{1,0:T(8,128)} fusion(bf16[8192,1024]{1,0:T(8,128)(2,1)} %param.8, bf16[2048,8192]{1,0:T(8,128)(2,1)} %all-gather.5.cloned.1.call-done, s32[]{:T(128)S(6)} %select_n.140), kind=kOutput, calls=%fused_computation.2 | convolution fusion | flops 17179869184 | bytes 37748740 | tf_op jit(solution)/shard_map/dot_general | solution.py:142
  267.3 22.6 %collective-permute-done = bf16[1024,1024]{1,0:T(8,128)(2,1)S(1)} collective-permute-done((bf16[1024,1024]{1,0:T(8,128)(2,1)S(1)}, bf16[1024,1024]{1,0:T(8,128)(2,1)S(1)}, u32[]{:S(2)}, u32[]{:S(2)}) %collective-permute-start) | collective-permute-done | bytes 2097184 | tf_op jit(solution)/shard_map/ppermute | solution.py:141
  290.0 0.0 copy-start.2
  290.0 1.3 copy-done.2
  291.3 5.9 %rotate_rows.1 = bf16[8,1,128,1024]{3,2,1,0:T(8,128)(2,1)} custom-call(f32[8,128,1024]{2,1,0:T(8,128)} %bitcast.40, bf16[8,128,1024]{2,1,0:T(8,128)(2,1)} %bitcast.42, f32[8,1,128,128]{3,2,1,0:T(8,128)} %get-tuple-element.11.refs_2_, f32[8,1,128,128]{3,2,1,0:T(8,128)} %get-tuple-element.10.refs_3_), custom_call_target="tpu_custom_call" | custom-call | flops 6291456 | bytes 8388608 | tf_op jit(solution)/shard_map/rotate_rows/pallas_call | solution.py:67
  297.2 0.0 all-gather.7.cloned.1.call-done
  297.2 0.0 copy-start.1
  297.2 1.4 constant_dynamic-slice_fusion.1
  298.7 0.1 maximum_bitcast_fusion
  298.8 1.1 copy.24
  299.9 1.5 reshape_reshape.3
  301.3 0.0 copy-done.1
  (7 shorter events, 0.1 us)
Async XLA Ops:
  7.2 185.4 %copy-start = (bf16[8192,128]{1,0:T(8,128)(2,1)S(1)}, bf16[8192,128]{1,0:T(8,128)(2,1)}, u32[]{:S(2)}) copy-start(bf16[8192,128]{1,0:T(8,128)(2,1)} %param.9) | copy-start | bytes 6291460
  7.2 75.3 %copy-start.4 = (s32[8]{0:T(128)S(1)}, s32[8]{0:T(128)}, u32[]{:S(2)}) copy-start(s32[8]{0:T(128)} %param.11) | copy-start | bytes 100
  7.2 76.1 %copy-start.3 = (s32[1024]{0:T(1024)S(1)}, s32[1024]{0:T(1024)}, u32[]{:S(2)}) copy-start(s32[1024]{0:T(1024)} %param.10) | copy-start | bytes 12292
  7.2 185.3 %all-gather.5.cloned.1.call-start = ((), (), s32[]{:S(2)}) async-start(), calls=%async_computation | async-start | bytes 35651584 | tf_op jit(solution)/shard_map/all_gather | solution.py:99
  11.7 285.6 %all-gather.7.cloned.1.call-start = ((), (), s32[]{:S(2)}) async-start(), calls=%async_computation.1 | async-start | bytes 4456448 | tf_op jit(solution)/shard_map/all_gather | solution.py:155
  207.3 8.7 %collective-permute-start.1 = (bf16[1024,128]{1,0:T(8,128)(2,1)S(1)}, bf16[1024,128]{1,0:T(8,128)(2,1)S(1)}, u32[]{:S(2)}, u32[]{:S(2)}) collective-permute-start(bf16[1024,128]{1,0:T(8,128)(2,1)S(1)} %dynamic-slice_convert_fusion), channel_id=1, source_target_pairs={{0,1},{1,0},{2,3},{3,2},{4,5},{5,4},{6,7},{7,6},{8,9},{9,8},{10,11... | collective-permute-start | bytes 786440 | tf_op jit(solution)/shard_map/ppermute | solution.py:131
  242.4 47.5 %collective-permute-start = (bf16[1024,1024]{1,0:T(8,128)(2,1)S(1)}, bf16[1024,1024]{1,0:T(8,128)(2,1)S(1)}, u32[]{:S(2)}, u32[]{:S(2)}) collective-permute-start(bf16[1024,1024]{1,0:T(8,128)(2,1)S(1)} %fusion.6), channel_id=1, source_target_pairs={{0,1},{1,0},{2,3},{3,2},{4,5},{5,4},{6,7},{7,6},{8,9},{9,8},{10,11... | collective-permute-start | bytes 6291464 | tf_op jit(solution)/shard_map/ppermute | solution.py:141
  290.0 1.3 copy-start.2
  297.2 4.1 %copy-start.1 = (bf16[8192,128]{1,0:T(8,128)(2,1)S(1)}, bf16[8192,128]{1,0:T(8,128)(2,1)}, u32[]{:S(2)}) copy-start(bf16[8192,128]{1,0:T(8,128)(2,1)} %param.9) | copy-start | bytes 6291460
Sparse Core Ops, SparseCore 0:
  11.8 180.7 all-gather.4
  220.6 50.0 all-gather.6
